TPU v7x, 256 devices: a whole 4x4x8 slice. The times are simulated.
256 devices in a mesh: row: 16 (over x, y), col: 16 (over z, core).
Axes of the slice: x: 4, y: 4, z: 8, core: 2. Of those that a mesh axis runs over, the one named last changes fastest.
Arguments:
- values: bfloat16 [8192, 8192], P('row', 'col'), may hold values from 0.0001296997 to 0.12988281
- tile_mask: int32 [64, 64], P('row', 'col'), may hold values 0 or 1
- keep_mask: int32 [64, 64], P('row', 'col'), may hold values 0 or 1
- thr_index: int32 [8192], P('col'), may hold values from 0 to 9
Outputs:
- expanded: bfloat16 [8192, 8192], P('row', 'col')
All inputs are finite; a program needn't handle non-finite values. No bound on the sum of `tile_mask` or of `keep_mask` on one device may be relied on, other than what follows from the above.
Results may differ from a plain program's by a relative error of at most 0.0004.
Values may be sent and summed in bfloat16 or wider, within the bound.
A program may use at most 64 MiB of HBM per device.

v0:
```python
import jax
import jax.numpy as jnp
from jax import lax
from jax.sharding import Mesh
from jax.sharding import PartitionSpec as P

TB = 128
ROW = ("row_0", "row_1")


def over_axes(x, axes):
    for axis in axes:
        x = lax.psum(x, axis)
    return x


def on_device(values, tile_mask, keep_mask, thr_index):
    row_count, col_count = values.shape
    row_tiles = row_count // TB
    col_tiles = col_count // TB
    matrix = (
        values.reshape(row_tiles, TB, col_tiles, TB)
        * tile_mask[:, None, :, None].astype(jnp.bfloat16)
    ).reshape(row_count, col_count)
    kept_cells = jnp.broadcast_to(
        keep_mask[:, None, :, None].astype(jnp.float32), (row_tiles, TB, col_tiles, TB)
    ).reshape(row_count, col_count)
    order_all = row_count * lax.axis_size(ROW)
    thresholds = 0.125 * thr_index.astype(jnp.float32)
    col_panel = lax.all_gather(matrix, ROW, axis=0, tiled=True)
    product = jnp.dot(
        lax.all_gather(matrix, "col", axis=1, tiled=True),
        col_panel,
        preferred_element_type=jnp.float32,
    )
    outputs = []
    for phase_idx in range(col_tiles):
        lo_col = phase_idx * TB
        part_prod = product[:, lo_col : lo_col + TB]
        col_means = over_axes(jnp.sum(part_prod, axis=0), ROW) / order_all
        pruned = (
            jnp.maximum(part_prod - thresholds[lo_col : lo_col + TB] * col_means, 0.0)
            * kept_cells[:, lo_col : lo_col + TB]
        )
        col_totals = over_axes(jnp.sum(pruned, axis=0), ROW) / order_all
        outputs.append(pruned / jnp.maximum(col_totals, 0.1))
    result = jnp.concatenate(outputs, axis=1)
    return result.astype(jnp.bfloat16)


def solution(mesh):
    finer = Mesh(mesh.devices.reshape(4, 4, mesh.shape["col"]), ("row_0", "row_1", "col"))
    placed = (P(ROW, "col"), P(ROW, "col"), P(ROW, "col"), P("col"))
    return jax.shard_map(
        on_device, mesh=finer, in_specs=placed, out_specs=P(ROW, "col"), check_vma=False
    )
```

profile of v0, /device:TPU:2, one launch (start us, length us, event | category | flops | bytes accessed | tf_op | source)
XLA Modules:
  0.0 198.9 jit_solution(1561034129201004434)
XLA Ops:
  6.5 0.0 all-gather.3.cloned.1.call-start
  6.5 0.7 convert_element_type.12
  7.2 0.2 mul.41
  7.4 1.9 bitcast_multiply_fusion
  9.3 0.0 all-gather.3.cloned.1.call-update
  9.4 0.0 all-gather.5.cloned.1.call-start
  9.4 0.7 all-gather.5.cloned.1.call-update
  10.1 0.7 convert_element_type.14
  10.8 0.2 broadcast_in_dim.2
  11.0 0.1 copy.9
  11.1 0.7 convert_multiply_fusion
  11.8 56.5 %all-gather.3.cloned.1.call-done = bf16[512,8192]{1,0:T(8,128)(2,1)} async-done(((bf16[512,512]{1,0:T(8,128)(2,1)}), bf16[512,8192]{1,0:T(8,128)(2,1)}) %all-gather.3.cloned.1.call-update) | async-done | bytes 8388624 | tf_op jit(solution)/shard_map/all_gather | solution.py:32
  68.3 76.8 %all-gather.5.cloned.1.call-done = bf16[8192,512]{1,0:T(8,128)(2,1)} async-done(((bf16[512,512]{1,0:T(8,128)(2,1)}), bf16[8192,512]{1,0:T(8,128)(2,1)}) %all-gather.5.cloned.1.call-update) | async-done | bytes 8388624 | tf_op jit(solution)/shard_map/all_gather | solution.py:30
  145.1 9.4 %fusion.4 = f32[512,512]{1,0:T(8,128)S(1)} fusion(bf16[512,8192]{1,0:T(8,128)(2,1)} %all-gather.3.cloned.1.call-done, bf16[8192,512]{1,0:T(8,128)(2,1)} %all-gather.5.cloned.1.call-done), kind=kOutput, calls=%fused_computation.28 | convolution fusion | flops 4294967296 | bytes 17825792 | tf_op jit(solution)/shard_map/dot_general | solution.py:31
  154.6 0.1 slice_reduce_fusion.3
  154.7 8.6 %all-reduce.3 = (f32[128]{0:T(128)S(1)}, f32[128]{0:T(128)S(1)}, f32[128]{0:T(128)S(1)}, f32[128]{0:T(128)S(1)}) all-reduce(f32[128]{0:T(128)S(1)} %get-tuple-element.9, f32[128]{0:T(128)S(1)} %get-tuple-element.10, f32[128]{0:T(128)S(1)} %get-tuple-element.11, ...), channel_id=1, replica_groups=mesh['row_0'=4,'row_1'=4,'col'=16] {'row_0'}, use_global_device_ids=true, to_apply=%region_1.0 | all-reduce | flops 512 | bytes 4096 | tf_op jit(solution)/shard_map/psum | solution.py:13
  163.3 10.1 %all-reduce.1 = (f32[128]{0:T(128)S(1)}, f32[128]{0:T(128)S(1)}, f32[128]{0:T(128)S(1)}, f32[128]{0:T(128)S(1)}) all-reduce(f32[128]{0:T(128)S(1)} %get-tuple-element.25, f32[128]{0:T(128)S(1)} %get-tuple-element.26, f32[128]{0:T(128)S(1)} %get-tuple-element.27, ...), channel_id=1, replica_groups=mesh['row_0'=4,'row_1'=4,'col'=16] {'row_1'}, use_global_device_ids=true, to_apply=%region_2.0 | all-reduce | flops 512 | bytes 4096 | tf_op jit(solution)/shard_map/psum | solution.py:13
  173.4 0.2 fusion
  173.5 8.6 %all-reduce.2 = (f32[128]{0:T(128)S(1)}, f32[128]{0:T(128)S(1)}, f32[128]{0:T(128)S(1)}, f32[128]{0:T(128)S(1)}) all-reduce(f32[128]{0:T(128)S(1)} %get-tuple-element.6, f32[128]{0:T(128)S(1)} %get-tuple-element.7, f32[128]{0:T(128)S(1)} %get-tuple-element.8, ...), channel_id=1, replica_groups=mesh['row_0'=4,'row_1'=4,'col'=16] {'row_0'}, use_global_device_ids=true, to_apply=%region_22.0 | all-reduce | flops 512 | bytes 4096 | tf_op jit(solution)/shard_map/psum | solution.py:13
  182.1 8.9 %all-reduce = (f32[128]{0:T(128)S(1)}, f32[128]{0:T(128)S(1)}, f32[128]{0:T(128)S(1)}, f32[128]{0:T(128)S(1)}) all-reduce(f32[128]{0:T(128)S(1)} %get-tuple-element.21, f32[128]{0:T(128)S(1)} %get-tuple-element.22, f32[128]{0:T(128)S(1)} %get-tuple-element.23, ...), channel_id=1, replica_groups=mesh['row_0'=4,'row_1'=4,'col'=16] {'row_1'}, use_global_device_ids=true, to_apply=%region_23.0 | all-reduce | flops 512 | bytes 4096 | tf_op jit(solution)/shard_map/psum | solution.py:13
  191.1 0.2 divide_convert_fusion.3
  191.2 0.9 pad_maximum_fusion
  (3 shorter events, 0.0 us)
Async XLA Ops:
  6.5 61.8 %all-gather.3.cloned.1.call-start = ((), (), s32[]{:S(2)}) async-start(), calls=%async_computation | async-start | bytes 8912896 | tf_op jit(solution)/shard_map/all_gather | solution.py:32
  9.4 135.8 %all-gather.5.cloned.1.call-start = ((), (), s32[]{:S(2)}) async-start(), calls=%async_computation.1 | async-start | bytes 8912896 | tf_op jit(solution)/shard_map/all_gather | solution.py:30
Sparse Core Ops, SparseCore 0:
  9.5 58.7 all-gather.2
  70.7 74.3 all-gather.4
where the time goes:
time: 199 us
  waiting for transfers between devices  134 us (67%)
  blocking collectives  36.2 us (18%)
  between operations  13.4 us (7%)
  matrix products  9.44 us (5%)
  other arithmetic  5.27 us (3%)
    all_gather x1, waiting for transfers between devices, on_device(): col_panel = lax.all_gather(matrix, ROW, axis=0, tiled=True)  76.8 us
    all_gather x1, waiting for transfers between devices, on_device(): lax.all_gather(matrix, 'col', axis=1, tiled=True)  56.5 us
    psum x4, blocking collectives, over_axes(): x = lax.psum(x, axis)  36.2 us
    dot_general x1, matrix products, on_device(): jnp.dot(lax.all_gather(matrix, 'col', axis=1, tiled=True), col_panel, pre...  9.44 us
  transfers between devices with their start and end apart: 2, of which 2 were waited for; matrix products, arithmetic and copies ran while one was open for 1% of the time, Pallas kernels for 0%

commit v1 on v0

v1 whole, which is shorter than its diff:
```python
import jax
import jax.numpy as jnp
from jax import lax
from jax.experimental import pallas as pl
from jax.experimental.pallas import tpu as pltpu
from jax.sharding import PartitionSpec as P

TB = 128
BLK = 512
QR = 128
EXTRA = 16
NX = 4
NZ = 8
MESH = pl.DeviceIdType.MESH

XP = [(0, 0, 0), (0, 0, 1), (0, 0, 2), (0, 0, 3), (1, 0, 0), (1, 0, 2), (0, 1, 2), (0, 1, 3), (0, 3, 2), (0, 3, 3),
      (0, 2, 2), (0, 2, 3), (1, 1, 2), (1, 3, 2), (1, 2, 2)]
XM = [((-dx) % 4, (-dy) % 4, q ^ 1) for dx, dy, q in XP]
YP = [(dy, dx, q ^ 2) for dx, dy, q in XP]
YM = [(dy, dx, q ^ 2) for dx, dy, q in XM]
ZP = [(d, q) for d in range(3) for q in (0, 1, 2, 3)] + [(3, 0), (3, 1)]
ZM = [((-d) % 8, q ^ 2) for d, q in ZP]


def land(link, chunk):
    if link == "xp":
        return ((chunk[0] + 1) % 4, chunk[1], chunk[2])
    if link == "xm":
        return ((chunk[0] - 1) % 4, chunk[1], chunk[2])
    if link == "yp":
        return (chunk[0], (chunk[1] + 1) % 4, chunk[2])
    if link == "ym":
        return (chunk[0], (chunk[1] - 1) % 4, chunk[2])
    if link == "zp":
        return ((chunk[0] + 1) % 8, chunk[1])
    return ((chunk[0] - 1) % 8, chunk[1])


LINKS = {"xp": XP, "xm": XM, "yp": YP, "ym": YM, "zp": ZP, "zm": ZM}
ROUND_B = {(0, 0): -1}
for _link in ("xp", "xm", "yp", "ym"):
    for _r, _c in enumerate(LINKS[_link]):
        _l = land(_link, _c)
        ROUND_B[_l[:2]] = max(ROUND_B.get(_l[:2], -1), _r)
LAST = len(XP) - 1


def kernel(values_ref, tile_ref, keep_ref, thr_ref, out_ref, raw, abuf, bbuf, acc, own, pbuf, sbuf, tbuf,
           raw_sem, send_xy, send_z, send_d, send_small, recv_b, recv_a, recv_d, recv_p, recv_s, recv_t, ready):
    row, col = lax.axis_index("row"), lax.axis_index("col")
    x, y, z, core = row // 4, row % 4, col // 2, col % 2

    def at(dx, dy):
        return (((x + dx + 4) % 4) * 4 + (y + dy + 4) % 4, col)

    def along(dz, other):
        return (row, ((z + dz + 8) % 8) * 2 + (core + other) % 2)

    peer = {"xp": at(1, 0), "xm": at(-1, 0), "yp": at(0, 1), "ym": at(0, -1), "zp": along(1, 0), "zm": along(-1, 0)}
    partner = along(0, 1)
    neighbours = list(peer.values()) + [partner]

    barrier = pltpu.get_barrier_semaphore()
    for n in neighbours:
        pl.semaphore_signal(barrier, inc=1, device_id=n, device_id_type=MESH)
    fetch = pltpu.make_async_copy(values_ref, raw, raw_sem)
    fetch.start()
    acc[...] = jnp.zeros_like(acc)
    fetch.wait()
    sums = [jnp.zeros((1, TB), jnp.float32) for _ in range(4)]
    for i in range(4):
        for j in range(4):
            tile = raw[pl.ds(i * TB, TB), pl.ds(j * TB, TB)].astype(jnp.float32) * tile_ref[i, j].astype(jnp.float32)
            sums[j] = sums[j] + jnp.sum(tile, axis=0, keepdims=True)
            tile = tile.astype(jnp.bfloat16)
            abuf[0, pl.ds(i * TB, TB), pl.ds(j * TB, TB)] = tile
            bbuf[0, pl.ds(i * TB, TB), pl.ds(j * TB, TB)] = tile
    for j in range(4):
        pbuf[0, :, pl.ds(j * TB, TB)] = sums[j]
    pl.semaphore_wait(barrier, len(neighbours))

    def quarter(buf, slot, q):
        return buf.at[slot, pl.ds(q * QR, QR), :]

    have = {("b", 0, 0, q) for q in range(4)} | {("a", 0, q) for q in range(4)}
    nxt = dict.fromkeys(LINKS, 0)
    sent = {"xy": [], "z": [], "d": [], "small": []}

    def advance():
        more = True
        while more:
            more = False
            for link, chunks in LINKS.items():
                if nxt[link] == len(chunks):
                    continue
                c = chunks[nxt[link]]
                kind = "a" if link[0] == "z" else "b"
                if (kind,) + c not in have:
                    continue
                to = land(link, c)
                if kind == "b":
                    src, dst = quarter(bbuf, c[0] * 4 + c[1], c[2]), quarter(bbuf, to[0] * 4 + to[1], to[2])
                    ss, rs = send_xy.at[len(sent["xy"])], recv_b.at[to[0] * 4 + to[1], to[2]]
                else:
                    src, dst = quarter(abuf, c[0] * 2, c[1]), quarter(abuf, to[0] * 2, to[1])
                    ss, rs = send_z.at[len(sent["z"])], recv_a.at[to[0], to[1]]
                copy = pltpu.make_async_remote_copy(src, dst, ss, rs, device_id=peer[link], device_id_type=MESH)
                copy.start()
                sent["xy" if kind == "b" else "z"].append(copy)
                nxt[link] += 1
                more = True

    def half(slot, h):
        return abuf.at[slot, pl.ds(h * 256, 256), :]

    def hand_over(dz, h):
        copy = pltpu.make_async_remote_copy(half(dz * 2, h), half(dz * 2 + 1, h), send_d.at[len(sent["d"])],
                                            recv_d.at[dz, h], device_id=partner, device_id_type=MESH)
        copy.start()
        sent["d"].append(copy)

    def take_over(dz):
        for h in range(2):
            pltpu.make_async_remote_copy(half(dz * 2, h), half(dz * 2 + 1, h), send_d.at[0], recv_d.at[dz, h],
                                         device_id=partner, device_id_type=MESH).wait_recv()

    handed = set()

    def arrive(r):
        for link, chunks in LINKS.items():
            if r >= len(chunks):
                continue
            to = land(link, chunks[r])
            if link[0] == "z":
                ref = quarter(abuf, to[0] * 2, to[1])
                sem = recv_a.at[to[0], to[1]]
                have.add(("a",) + to)
            else:
                ref = quarter(bbuf, to[0] * 4 + to[1], to[2])
                sem = recv_b.at[to[0] * 4 + to[1], to[2]]
                have.add(("b",) + to)
            pltpu.make_async_remote_copy(ref, ref, send_d.at[0], sem, device_id=partner,
                                         device_id_type=MESH).wait_recv()
            advance()
            if link[0] == "z":
                for h in range(2):
                    if (to[0], h) not in handed and all(("a", to[0], 2 * h + k) in have for k in range(2)):
                        handed.add((to[0], h))
                        hand_over(to[0], h)

    def greet(i):
        for n in neighbours:
            pl.semaphore_signal(ready.at[i], inc=1, device_id=n, device_id_type=MESH)
        pl.semaphore_wait(ready.at[i], len(neighbours))

    def small(src, dst, sem, to):
        copy = pltpu.make_async_remote_copy(src, dst, send_small.at[len(sent["small"])], sem, device_id=to,
                                            device_id_type=MESH)
        copy.start()
        sent["small"].append(copy)

    def small_wait(ref, sem):
        pltpu.make_async_remote_copy(ref, ref, send_d.at[0], sem, device_id=partner, device_id_type=MESH).wait_recv()

    def left_slot(i):
        origin = ((x - i // 4 + 4) % 4) * 4 + (y - i % 4 + 4) % 4
        dz = (z - origin // 2 + 8) % 8
        return dz, (origin % 2 + core) % 2

    def multiply(i):
        dz, other = left_slot(i)
        acc[...] += jnp.dot(abuf[dz * 2 + other], bbuf[i], preferred_element_type=jnp.float32)

    def round_of(i):
        dz, other = left_slot(i)
        far = jnp.minimum(dz, 8 - dz)
        ra = jnp.minimum(4 * far - 1, 13) + other
        rb = jnp.int32(-1)
        for (dx, dy), r in ROUND_B.items():
            rb = jnp.where(i == dx * 4 + dy, jnp.int32(r), rb)
        return jnp.maximum(ra, rb)

    def multiply_ready(lo, hi):
        def step(i, carry):
            r = round_of(i)

            @pl.when((r >= lo) & (r < hi))
            def _():
                multiply(i)

            return carry

        lax.fori_loop(0, 16, step, 0)

    advance()
    for h in range(2):
        handed.add((0, h))
        hand_over(0, h)
    for i in range(3):
        greet(i)
    for a in range(4):
        for b in range(4):
            if (a, b) != (0, 0):
                small(pbuf.at[0], pbuf.at[a * 4 + b], recv_p.at[a * 4 + b], at(a, b))
    greet(3)
    arrive(0)
    for s in range(1, 16):
        small_wait(pbuf.at[s], recv_p.at[s])
    own_s = pbuf[0]
    for s in range(1, 16):
        own_s = own_s + pbuf[s]
    sbuf[0] = own_s
    arrive(1)
    for d in range(8):
        for other in range(2):
            if (d, other) != (0, 0):
                small(sbuf.at[0], sbuf.at[d * 2 + other], recv_s.at[d * 2 + other], along(d, other))
    arrive(2)
    arrive(3)
    for s in range(1, 16):
        small_wait(sbuf.at[s], recv_s.at[s])
    for s in range(16):
        v = sbuf[s]
        p0 = v.astype(jnp.bfloat16).astype(jnp.float32)
        p1 = (v - p0).astype(jnp.bfloat16).astype(jnp.float32)
        p2 = v - p0 - p1
        rows = lax.broadcasted_iota(jnp.int32, (EXTRA, BLK), 0)
        block = jnp.where(rows == 0, p0, jnp.where(rows == 1, p1, jnp.where(rows == 2, p2, 0.0)))
        abuf[s, pl.ds(BLK, EXTRA), :] = block.astype(jnp.bfloat16)
    take_over(0)
    multiply_ready(-2, 4)
    done = 4
    for r in range(4, 14):
        arrive(r)
        if r == 4:
            take_over(1)
            take_over(7)
        if r == 8:
            take_over(2)
            take_over(6)
        if r == 12:
            take_over(3)
            take_over(5)
        if r in (5, 7, 9, 11, 12, 13):
            multiply_ready(done, r + 1)
            done = r + 1
    take_over(4)
    far = ((z + 4) % 8) * 2 + (core + 1) % 2
    far_slot = ((x - far // 4 + 4) % 4) * 4 + (y - far % 4 + 4) % 4

    @pl.when(far_slot != 10)
    def _():
        multiply(far_slot)

    arrive(14)
    multiply(10)

    col_means = (acc[BLK : BLK + 1] + acc[BLK + 1 : BLK + 2] + acc[BLK + 2 : BLK + 3]) / (BLK * 16)
    cut = 0.125 * thr_ref[...].astype(jnp.float32) * col_means
    for j in range(4):
        total = jnp.zeros((1, TB), jnp.float32)
        for i in range(4):
            part = acc[pl.ds(i * TB, TB), pl.ds(j * TB, TB)]
            part = jnp.maximum(part - cut[:, j * TB : (j + 1) * TB], 0.0) * keep_ref[i, j].astype(jnp.float32)
            acc[pl.ds(i * TB, TB), pl.ds(j * TB, TB)] = part
            total = total + jnp.sum(part, axis=0, keepdims=True)
        tbuf[0, :, pl.ds(j * TB, TB)] = total
    for a in range(4):
        for b in range(4):
            if (a, b) != (0, 0):
                small(tbuf.at[0], tbuf.at[a * 4 + b], recv_t.at[a * 4 + b], at(a, b))
    for group in sent.values():
        for copy in group:
            copy.wait_send()
    total = tbuf[0]
    for s in range(1, 16):
        small_wait(tbuf.at[s], recv_t.at[s])
        total = total + tbuf[s]
    scale = jnp.maximum(total / (BLK * 16), 0.1)
    out_ref[...] = (acc[:BLK] / scale).astype(jnp.bfloat16)


def on_device(values, tile_mask, keep_mask, thr_index):
    dma = pltpu.SemaphoreType.DMA
    return pl.pallas_call(
        kernel,
        out_shape=jax.ShapeDtypeStruct(values.shape, jnp.bfloat16),
        in_specs=[
            pl.BlockSpec(memory_space=pl.ANY),
            pl.BlockSpec(memory_space=pltpu.SMEM),
            pl.BlockSpec(memory_space=pltpu.SMEM),
            pl.BlockSpec(memory_space=pltpu.VMEM),
        ],
        out_specs=pl.BlockSpec(memory_space=pltpu.VMEM),
        scratch_shapes=[
            pltpu.VMEM((BLK, BLK), jnp.bfloat16),
            pltpu.VMEM((16, BLK + EXTRA, BLK), jnp.bfloat16),
            pltpu.VMEM((16, BLK, BLK), jnp.bfloat16),
            pltpu.VMEM((BLK + EXTRA, BLK), jnp.float32),
            pltpu.VMEM((1, BLK), jnp.float32),
            pltpu.VMEM((16, 1, BLK), jnp.float32),
            pltpu.VMEM((16, 1, BLK), jnp.float32),
            pltpu.VMEM((16, 1, BLK), jnp.float32),
            dma,
            dma((60,)),
            dma((28,)),
            dma((16,)),
            dma((45,)),
            dma((16, 4)),
            dma((8, 4)),
            dma((8, 2)),
            dma((16,)),
            dma((16,)),
            dma((16,)),
            pltpu.SemaphoreType.REGULAR((4,)),
        ],
        compiler_params=pltpu.CompilerParams(collective_id=0, has_side_effects=True, vmem_limit_bytes=48 << 20),
    )(values, tile_mask, keep_mask, thr_index.reshape(1, BLK))


def solution(mesh):
    placed = (P("row", "col"), P("row", "col"), P("row", "col"), P("col"))
    return jax.shard_map(on_device, mesh=mesh, in_specs=placed, out_specs=P("row", "col"), check_vma=False)
```

time: 199 us -> 68.5 us (0.34)
  the two profiles are of different devices: /device:TPU:2 before, /device:TPU:1 now
where the time goes in v1:
time: 68.5 us; the launch traced here: 68.3 us
  Pallas kernels  64.4 us (94%)
  local copies, waits for them, and re-layouts  3.88 us (6%)
    pallas_call x1, Pallas kernels, on_device(): pl.pallas_call(kernel, out_shape=jax.ShapeDtypeStruct(values.shape, jnp.b...  64.4 us
    unnamed x9, local copies, waits for them, and re-layouts  3.88 us

profile of v1, /device:TPU:1, one launch (start us, length us, event | category | flops | bytes accessed | tf_op | source)
XLA Modules:
  0.0 68.3 jit_solution(13757002875177326732)
XLA Ops:
  0.0 0.0 copy-start
  0.0 1.0 %copy-done = bf16[512,512]{1,0:T(8,128)(2,1)S(1)} copy-done((bf16[512,512]{1,0:T(8,128)(2,1)S(1)}, bf16[512,512]{1,0:T(8,128)(2,1)}, u32[]{:S(2)}) %copy-start) | copy-done | bytes 524312
  1.0 0.0 copy-start.1
  1.0 0.7 copy-done.1
  1.7 0.0 copy-start.2
  1.7 0.7 copy-done.2
  2.4 0.0 copy-start.3
  2.4 0.7 copy-done.3
  3.1 64.4 %shard_map.46 = bf16[512,512]{1,0:T(8,128)(2,1)S(1)} custom-call(bf16[512,512]{1,0:T(8,128)(2,1)S(1)} %copy-done, s32[4,4]{1,0:T(4,128)S(1)} %copy-done.1, s32[4,4]{1,0:T(4,128)S(1)} %copy-done.2, s32[1,512]{1,0:T(1,128)S(1)} %bitcast.1), custom_call_target="tpu_custom_call" | custom-call | tf_op jit(solution)/shard_map/pallas_call | solution.py:285
  67.5 0.8 %copy.6 = bf16[512,512]{1,0:T(8,128)(2,1)} copy(bf16[512,512]{1,0:T(8,128)(2,1)S(1)} %shard_map.46) | data formatting | bytes 1048576
Async XLA Ops:
  0.0 1.0 %copy-start = (bf16[512,512]{1,0:T(8,128)(2,1)S(1)}, bf16[512,512]{1,0:T(8,128)(2,1)}, u32[]{:S(2)}) copy-start(bf16[512,512]{1,0:T(8,128)(2,1)} %values_ref.1) | copy-start | bytes 1572868
  1.0 0.7 copy-start.1
  1.7 0.7 copy-start.2
  2.4 0.7 copy-start.3

commit v2 on v1

--- a/solution.py
+++ b/solution.py
@@ -45,7 +45,7 @@
 LAST = len(XP) - 1
 
 
-def kernel(values_ref, tile_ref, keep_ref, thr_ref, out_ref, raw, abuf, bbuf, acc, own, pbuf, sbuf, tbuf,
+def kernel(values_ref, tile_hbm, keep_hbm, thr_hbm, out_ref, raw, tile_ref, keep_ref, thr_ref, abuf, bbuf, acc, own, pbuf, sbuf, tbuf,
            raw_sem, send_xy, send_z, send_d, send_small, recv_b, recv_a, recv_d, recv_p, recv_s, recv_t, ready):
     row, col = lax.axis_index("row"), lax.axis_index("col")
     x, y, z, core = row // 4, row % 4, col // 2, col % 2
@@ -63,10 +63,17 @@
     barrier = pltpu.get_barrier_semaphore()
     for n in neighbours:
         pl.semaphore_signal(barrier, inc=1, device_id=n, device_id_type=MESH)
-    fetch = pltpu.make_async_copy(values_ref, raw, raw_sem)
-    fetch.start()
+    fetches = [
+        pltpu.make_async_copy(src, dst, raw_sem.at[i])
+        for i, (src, dst) in enumerate(
+            [(tile_hbm, tile_ref), (values_ref, raw), (keep_hbm, keep_ref), (thr_hbm, thr_ref)]
+        )
+    ]
+    for fetch in fetches:
+        fetch.start()
     acc[...] = jnp.zeros_like(acc)
-    fetch.wait()
+    for fetch in fetches:
+        fetch.wait()
     sums = [jnp.zeros((1, TB), jnp.float32) for _ in range(4)]
     for i in range(4):
         for j in range(4):
@@ -285,15 +292,13 @@
     return pl.pallas_call(
         kernel,
         out_shape=jax.ShapeDtypeStruct(values.shape, jnp.bfloat16),
-        in_specs=[
-            pl.BlockSpec(memory_space=pl.ANY),
-            pl.BlockSpec(memory_space=pltpu.SMEM),
-            pl.BlockSpec(memory_space=pltpu.SMEM),
-            pl.BlockSpec(memory_space=pltpu.VMEM),
-        ],
+        in_specs=[pl.BlockSpec(memory_space=pltpu.HBM)] * 4,
         out_specs=pl.BlockSpec(memory_space=pltpu.VMEM),
         scratch_shapes=[
             pltpu.VMEM((BLK, BLK), jnp.bfloat16),
+            pltpu.SMEM((4, 4), jnp.int32),
+            pltpu.SMEM((4, 4), jnp.int32),
+            pltpu.VMEM((1, BLK), jnp.int32),
             pltpu.VMEM((16, BLK + EXTRA, BLK), jnp.bfloat16),
             pltpu.VMEM((16, BLK, BLK), jnp.bfloat16),
             pltpu.VMEM((BLK + EXTRA, BLK), jnp.float32),
@@ -301,7 +306,7 @@
             pltpu.VMEM((16, 1, BLK), jnp.float32),
             pltpu.VMEM((16, 1, BLK), jnp.float32),
             pltpu.VMEM((16, 1, BLK), jnp.float32),
-            dma,
+            dma((4,)),
             dma((60,)),
             dma((28,)),
             dma((16,)),
@@ -315,7 +320,7 @@
             pltpu.SemaphoreType.REGULAR((4,)),
         ],
         compiler_params=pltpu.CompilerParams(collective_id=0, has_side_effects=True, vmem_limit_bytes=48 << 20),
-    )(values, tile_mask, keep_mask, thr_index.reshape(1, BLK))
+    )(*[pltpu.with_memory_space_constraint(v, pltpu.HBM) for v in (values, tile_mask, keep_mask, thr_index.reshape(1, BLK))])
 
 
 def solution(mesh):

time: 68.5 us -> 64.7 us (0.945)
  local copies, waits for them, and re-layouts: 3.88 us -> 0.8 us
    unnamed x9 -> x1, local copies, waits for them, and re-layouts: 3.88 us -> 0.8 us
where the time goes in v2:
time: 64.7 us; the launch traced here: 64.6 us
  Pallas kernels  63.8 us (99%)
  local copies, waits for them, and re-layouts  0.8 us (1%)
    pallas_call x1, Pallas kernels, on_device(): pl.pallas_call(kernel, out_shape=jax.ShapeDtypeStruct(values.shape, jnp.b...  63.8 us

profile of v2, /device:TPU:1, one launch (start us, length us, event | category | flops | bytes accessed | tf_op | source)
XLA Modules:
  0.0 64.6 jit_solution(3785765384349956299)
XLA Ops:
  0.0 63.8 %shard_map.46 = bf16[512,512]{1,0:T(8,128)(2,1)S(1)} custom-call(bf16[512,512]{1,0:T(8,128)(2,1)} %values_ref.1, s32[4,4]{1,0:T(4,128)} %tile_hbm.1, s32[4,4]{1,0:T(4,128)} %keep_hbm.1, s32[1,512]{1,0:T(1,128)} %bitcast.1), custom_call_target="tpu_custom_call" | custom-call | tf_op jit(solution)/shard_map/pallas_call | solution.py:292
  63.8 0.8 %copy.6 = bf16[512,512]{1,0:T(8,128)(2,1)} copy(bf16[512,512]{1,0:T(8,128)(2,1)S(1)} %shard_map.46) | data formatting | bytes 1048576

commit v3 on v0

v3 whole, which is shorter than its diff:
```python
import jax
import jax.numpy as jnp
from jax import lax
from jax.experimental import pallas as pl
from jax.experimental.pallas import tpu as pltpu
from jax.sharding import PartitionSpec as P

TB = 128
BLK = 512
QR = 128
NX = 4
NZ = 8
MESH = pl.DeviceIdType.MESH

OWN = [(0, 0, 0), (0, 0, 1), (0, 0, 2), (0, 0, 3)]
XP = OWN + [(1, 0, 0), (1, 0, 2), (0, 1, 2), (0, 1, 3), (0, 3, 2), (0, 3, 3), (0, 2, 2), (0, 2, 3), (1, 1, 2), (1, 3, 2),
            (1, 2, 2)]
XM = OWN + [((-dx) % 4, dy, q ^ 1) for dx, dy, q in XP[4:]]
YP = OWN + [(dy, dx, q ^ 2) for dx, dy, q in [XP[5], XP[4]] + XP[6:]]
YM = OWN + [(dy, dx, q ^ 2) for dx, dy, q in [XM[5], XM[4]] + XM[6:]]
ZP = [(d, q) for d in (0, 1, 2) for q in range(4)] + [(3, 0), (3, 1)]
ZM = [(d, q) for d in (0, 7, 6) for q in range(4)] + [(5, 2), (5, 3)]
LINKS = {"xp": XP, "xm": XM, "yp": YP, "ym": YM, "zp": ZP, "zm": ZM}
STEP = {"xp": (1, 0, 0), "xm": (3, 0, 0), "yp": (0, 1, 0), "ym": (0, 3, 0), "zp": (1, 0), "zm": (7, 0)}


def land(link, chunk):
    extent = 8 if link[0] == "z" else 4
    moved = [(a + b) % extent for a, b in zip(chunk, STEP[link])]
    return tuple(moved[:-1]) + (chunk[-1],)


EVENT_OF_ROUND = [0, 0, 0, 0, 1, 1, 2, 2, 3, 3, 4, 4, 5, 6, 7]
EVENT_B = [0] * 16
for _link in ("xp", "xm", "yp", "ym"):
    for _r, _c in enumerate(LINKS[_link]):
        _l = land(_link, _c)
        EVENT_B[_l[0] * 4 + _l[1]] = max(EVENT_B[_l[0] * 4 + _l[1]], EVENT_OF_ROUND[_r])
EVENT_A = [0, 0, 1, 2, 3, 4, 6, 7, 8, 9, 5, 7, 3, 4, 1, 2]


def kernel(values_ref, tile_hbm, keep_hbm, thr_hbm, out_ref, raw, tile_ref, keep_ref, thr_ref, abuf, bbuf, acc, pbuf, sbuf,
           vbuf, tbuf, raw_sem, send_xy, send_z, send_d, send_p, send_s, send_v, send_t, recv_b, recv_a, recv_d, recv_p,
           recv_s, recv_v, recv_t, go, ready):
    row, col = lax.axis_index("row"), lax.axis_index("col")
    x, y, z, core = row // 4, row % 4, col // 2, col % 2

    def at(dx, dy):
        return (((x + dx + 4) % 4) * 4 + (y + dy + 4) % 4, col)

    def along(dz, other):
        return (row, ((z + dz + 8) % 8) * 2 + (core + other) % 2)

    def signal(sem, to):
        pl.semaphore_signal(sem, inc=1, device_id=to, device_id_type=MESH)

    peer = {"xp": at(1, 0), "xm": at(-1, 0), "yp": at(0, 1), "ym": at(0, -1), "zp": along(1, 0), "zm": along(-1, 0)}
    partner = along(0, 1)
    plane = [peer[link] for link in ("xp", "xm", "yp", "ym")]
    line = [peer["zp"], peer["zm"]]
    late_p = (z % 4) // 3
    late_m = (3 - z % 4) // 3
    late = late_p + late_m

    barrier = pltpu.get_barrier_semaphore()
    for to in plane:
        signal(barrier, (to[0], z * 2))
    signal(barrier, (row, ((z + 1) % 8) * 2 + late_p))
    signal(barrier, (row, ((z + 7) % 8) * 2 + late_m))

    @pl.when(core == 1)
    def _():
        signal(barrier, partner)

    tiles = pltpu.make_async_copy(tile_hbm, tile_ref, raw_sem.at[0])
    tiles.start()
    fetches = [
        pltpu.make_async_copy(
            values_ref.at[pl.ds(i * QR, QR), :], raw.at[pl.ds(i * QR, QR), :], raw_sem.at[1 + i]
        )
        for i in range(4)
    ]
    for fetch in fetches:
        fetch.start()
    rest = [
        pltpu.make_async_copy(keep_hbm, keep_ref, raw_sem.at[5]),
        pltpu.make_async_copy(thr_hbm, thr_ref, raw_sem.at[6]),
    ]
    for fetch in rest:
        fetch.start()

    def mask(i):
        fetches[i].wait()
        for j in range(4):
            tile = raw[pl.ds(i * TB, TB), pl.ds(j * TB, TB)].astype(jnp.float32) * tile_ref[i, j].astype(jnp.float32)
            tile = tile.astype(jnp.bfloat16)
            abuf[0, pl.ds(i * TB, TB), pl.ds(j * TB, TB)] = tile
            bbuf[0, pl.ds(i * TB, TB), pl.ds(j * TB, TB)] = tile

    sent = []

    def remote(src, dst, ss, rs, to):
        return pltpu.make_async_remote_copy(src, dst, ss, rs, device_id=to, device_id_type=MESH)

    def arrived(ref, sem):
        remote(ref, ref, send_d.at[0], sem, partner).wait_recv()

    def quarter(buf, slot, q):
        return buf.at[slot, pl.ds(q * QR, QR), :]

    def half(slot, h):
        return abuf.at[slot, pl.ds(h * 256, 256), :]

    have = set()
    nxt = dict.fromkeys(("xp", "xm", "yp", "ym"), 0)
    n_xy = [0]

    def advance():
        more = True
        while more:
            more = False
            for link in nxt:
                if nxt[link] == len(LINKS[link]) or LINKS[link][nxt[link]] not in have:
                    continue
                c = LINKS[link][nxt[link]]
                to = land(link, c)
                copy = remote(
                    quarter(bbuf, c[0] * 4 + c[1], c[2]),
                    quarter(bbuf, to[0] * 4 + to[1], to[2]),
                    send_xy.at[n_xy[0]],
                    recv_b.at[to[0] * 4 + to[1], to[2]],
                    peer[link],
                )
                copy.start()
                sent.append(copy)
                n_xy[0] += 1
                nxt[link] += 1
                more = True

    def along_xy(r):
        for link in nxt:
            to = land(link, LINKS[link][r])
            arrived(quarter(bbuf, to[0] * 4 + to[1], to[2]), recv_b.at[to[0] * 4 + to[1], to[2]])
            have.add(to)
            advance()

    def z_copy(link, c, slot):
        to = land(link, c)
        return remote(
            quarter(abuf, c[0] * 2, c[1]), quarter(abuf, to[0] * 2, to[1]), send_z.at[slot], recv_a.at[to[0], to[1]], peer[link]
        )

    def send_along_z(link, r):
        z_copy(link, LINKS[link][r], r if link == "zp" else 14 + r).start()

    def hand_over(dz, h):
        copy = remote(half(dz * 2, h), half(dz * 2 + 1, h), send_d.at[dz * 2 + h], recv_d.at[dz, h], partner)
        copy.start()
        sent.append(copy)

    def take_over(dz):
        for h in range(2):
            arrived(half(dz * 2 + 1, h), recv_d.at[dz, h])

    def along_z(link, r):
        to = land(link, LINKS[link][r])
        arrived(quarter(abuf, to[0] * 2, to[1]), recv_a.at[to[0], to[1]])
        if to in LINKS[link]:
            n = LINKS[link].index(to)
            if link == "zp" and n == 13:
                @pl.when(z != 7)
                def _():
                    send_along_z(link, n)

            else:
                send_along_z(link, n)
        elif link == "zm" and to == (5, 1):

            @pl.when(z == 1)
            def _():
                z_copy(link, to, 28).start()

        if r % 2 == 1:
            hand_over(to[0], to[1] // 2)

    def own_along_z(q):
        @pl.when(late_p == 0)
        def _():
            send_along_z("zp", q)

        @pl.when(late_m == 0)
        def _():
            send_along_z("zm", q)

    def across(when):
        @pl.when(when & (late > 0))
        def _():
            @pl.when(core == 1)
            def _():
                pl.semaphore_wait(barrier, 2 * late)
                signal(go.at[1], partner)

            @pl.when(core == 0)
            def _():
                pl.semaphore_wait(go.at[1], 1)

            for link, edge in (("zp", late_p), ("zm", late_m)):

                @pl.when(edge > 0)
                def _():
                    for r in range(4):
                        send_along_z(link, r)

    def greet(i, who):
        for to in who:
            signal(ready.at[i], to)

    def met(i, who):
        pl.semaphore_wait(ready.at[i], len(who))

    def left_slot(i):
        origin = ((x - i // 4 + 4) % 4) * 4 + (y - i % 4 + 4) % 4
        return ((z - origin // 2 + 8) % 8) * 2 + (origin % 2 + core) % 2

    def right_slot(a):
        origin = ((z - a // 2 + 8) % 8) * 2 + (core + a % 2) % 2
        return ((x - origin // 4 + 4) % 4) * 4 + (y - origin % 4 + 4) % 4

    def pick(table, i):
        value = jnp.int32(table[0])
        for k in range(1, len(table)):
            if table[k] != table[0]:
                value = jnp.where(i == k, jnp.int32(table[k]), value)
        return value

    def multiply(a, i):
        acc[...] += jnp.dot(abuf[a], bbuf[i], preferred_element_type=jnp.float32)

    def event(e):
        todo = []
        for i in range(16):
            if EVENT_B[i] == e:
                a = left_slot(i)
                todo.append((a, jnp.int32(i), pick(EVENT_A, a) <= e))
        for a in range(16):
            if EVENT_A[a] == e:
                i = right_slot(a)
                todo.append((jnp.int32(a), i, pick(EVENT_B, i) < e))

        def step(t, carry):
            a, i, ok = todo[0]
            ok = ok.astype(jnp.int32)
            for k in range(1, len(todo)):
                a = jnp.where(t == k, todo[k][0], a)
                i = jnp.where(t == k, todo[k][1], i)
                ok = jnp.where(t == k, todo[k][2].astype(jnp.int32), ok)

            @pl.when(ok > 0)
            def _():
                multiply(a, i)

            return carry

        lax.fori_loop(0, len(todo), step, 0)

    def to_plane(src, dst, send, recv):
        for a in range(4):
            for b in range(4):
                if (a, b) != (0, 0):
                    copy = remote(src, dst.at[a * 4 + b], send.at[a * 4 + b], recv.at[a * 4 + b], at(a, b))
                    copy.start()
                    sent.append(copy)

    tiles.wait()
    mask(0)

    @pl.when(core == 0)
    def _():
        pl.semaphore_wait(barrier, 13 - 2 * late)
        signal(go.at[0], partner)

    @pl.when(core == 1)
    def _():
        pl.semaphore_wait(go.at[0], 1)

    for i in range(4):
        if i:
            mask(i)
        have.add((0, 0, i))
        advance()
        own_along_z(i)
        if i % 2:
            hand_over(0, i // 2)
    across(z != 0)
    greet(0, plane)
    acc[...] = jnp.zeros_like(acc)
    own_sum = jnp.zeros((1, BLK), jnp.float32)
    for i in range(4):
        own_sum = own_sum + jnp.sum(bbuf[0, pl.ds(i * TB, TB), :].astype(jnp.float32), axis=0, keepdims=True)
    pbuf[0] = own_sum
    for i in range(1, 3):
        met(i - 1, plane)
        greet(i, plane)
    met(2, plane)
    root = z * 2 + core
    slot = ((root // 4 - x + 4) % 4) * 4 + (root % 4 - y + 4) % 4
    is_root = slot == 0
    to_root = remote(pbuf.at[0], pbuf.at[slot], send_p, recv_p.at[slot], (root, col))

    @pl.when(slot != 0)
    def _():
        to_root.start()

    across(z == 0)
    greet(3, line)
    along_xy(0)
    along_xy(1)
    along_z("zm", 0)
    along_xy(2)
    along_z("zm", 1)
    along_z("zp", 0)
    met(3, line)
    greet(4, line)
    along_xy(3)
    along_z("zm", 2)
    along_z("zp", 1)
    take_over(0)
    event(0)

    @pl.when(is_root)
    def _():
        total = pbuf[0]
        for k in range(1, 16):
            arrived(pbuf.at[k], recv_p.at[k])
            total = total + pbuf[k]
        sbuf[0] = total

    for r in range(4, 15):
        along_xy(r)
        along_z("zm", r - 1)
        if r < 14:
            along_z("zp", r - 2)
        if r == 5:
            met(4, line)
            greet(5, line)
        if r == 7:
            met(5, line)
            for k in range(1, 16):
                copy = remote(sbuf.at[0], sbuf.at[1], send_s.at[k], recv_s, along(k // 2, k % 2))

                @pl.when(is_root)
                def _():
                    copy.start()

        if r in (7, 11, 14):
            for dz in {7: (1, 7), 11: (2, 6), 14: (3, 5)}[r]:
                take_over(dz)
        if r in (5, 7, 9, 11, 12, 13, 14):
            event(EVENT_OF_ROUND[r])
        if r == 11:
            @pl.when(slot != 0)
            def _():
                arrived(sbuf.at[1], recv_s)

            v = jnp.where(is_root, sbuf[0], sbuf[1])
            p0 = v.astype(jnp.bfloat16).astype(jnp.float32)
            p1 = (v - p0).astype(jnp.bfloat16).astype(jnp.float32)
            p2 = v - p0 - p1
            rows = lax.broadcasted_iota(jnp.int32, (16, BLK), 0)
            parts = jnp.where(rows == 0, p0, jnp.where(rows == 1, p1, jnp.where(rows == 2, p2, 0.0)))
            own = jnp.dot(parts.astype(jnp.bfloat16), bbuf[0], preferred_element_type=jnp.float32)
            vbuf[0] = jnp.sum(own, axis=0, keepdims=True)
            to_plane(vbuf.at[0], vbuf, send_v, recv_v)
    along_z("zp", 12)
    along_z("zp", 13)
    event(8)
    for fetch in rest:
        fetch.wait()
    col_means = vbuf[0]
    for k in range(1, 16):
        arrived(vbuf.at[k], recv_v.at[k])
        col_means = col_means + vbuf[k]
    cut = 0.125 * thr_ref[...].astype(jnp.float32) * (col_means / (BLK * 16))
    take_over(4)
    event(9)

    for j in range(4):
        total = jnp.zeros((1, TB), jnp.float32)
        for i in range(4):
            part = acc[pl.ds(i * TB, TB), pl.ds(j * TB, TB)]
            part = jnp.maximum(part - cut[:, j * TB : (j + 1) * TB], 0.0) * keep_ref[i, j].astype(jnp.float32)
            acc[pl.ds(i * TB, TB), pl.ds(j * TB, TB)] = part
            total = total + jnp.sum(part, axis=0, keepdims=True)
        tbuf[0, :, pl.ds(j * TB, TB)] = total
    to_plane(tbuf.at[0], tbuf, send_t, recv_t)
    for copy in sent:
        copy.wait_send()
    for link in ("zp", "zm"):
        for r in range(14):
            if (link, r) != ("zp", 13):
                z_copy(link, LINKS[link][r], r if link == "zp" else 14 + r).wait_send()

    @pl.when(z != 7)
    def _():
        z_copy("zp", ZP[13], 13).wait_send()

    @pl.when(z == 1)
    def _():
        z_copy("zm", (5, 1), 28).wait_send()

    @pl.when(slot != 0)
    def _():
        to_root.wait_send()

    @pl.when(is_root)
    def _():
        for k in range(1, 16):
            remote(sbuf.at[0], sbuf.at[1], send_s.at[k], recv_s, along(k // 2, k % 2)).wait_send()

    total = tbuf[0]
    for k in range(1, 16):
        arrived(tbuf.at[k], recv_t.at[k])
        total = total + tbuf[k]
    scale = 1.0 / jnp.maximum(total / (BLK * 16), 0.1)
    out_ref[...] = (acc[...] * scale).astype(jnp.bfloat16)


def on_device(values, tile_mask, keep_mask, thr_index):
    dma = pltpu.SemaphoreType.DMA
    return pl.pallas_call(
        kernel,
        out_shape=jax.ShapeDtypeStruct(values.shape, jnp.bfloat16),
        in_specs=[pl.BlockSpec(memory_space=pltpu.HBM)] * 4,
        out_specs=pl.BlockSpec(memory_space=pltpu.VMEM),
        scratch_shapes=[
            pltpu.VMEM((BLK, BLK), jnp.bfloat16),
            pltpu.SMEM((4, 4), jnp.int32),
            pltpu.SMEM((4, 4), jnp.int32),
            pltpu.VMEM((1, BLK), jnp.int32),
            pltpu.VMEM((16, BLK, BLK), jnp.bfloat16),
            pltpu.VMEM((16, BLK, BLK), jnp.bfloat16),
            pltpu.VMEM((BLK, BLK), jnp.float32),
            pltpu.VMEM((16, 1, BLK), jnp.float32),
            pltpu.VMEM((2, 1, BLK), jnp.float32),
            pltpu.VMEM((16, 1, BLK), jnp.float32),
            pltpu.VMEM((16, 1, BLK), jnp.float32),
            dma((7,)),
            dma((60,)),
            dma((29,)),
            dma((16,)),
            dma,
            dma((16,)),
            dma((16,)),
            dma((16,)),
            dma((16, 4)),
            dma((8, 4)),
            dma((8, 2)),
            dma((16,)),
            dma,
            dma((16,)),
            dma((16,)),
            pltpu.SemaphoreType.REGULAR((2,)),
            pltpu.SemaphoreType.REGULAR((6,)),
        ],
        compiler_params=pltpu.CompilerParams(collective_id=0, has_side_effects=True, vmem_limit_bytes=48 << 20),
    )(*[pltpu.with_memory_space_constraint(v, pltpu.HBM) for v in (values, tile_mask, keep_mask, thr_index.reshape(1, BLK))])


def solution(mesh):
    placed = (P("row", "col"), P("row", "col"), P("row", "col"), P("col"))
    return jax.shard_map(on_device, mesh=mesh, in_specs=placed, out_specs=P("row", "col"), check_vma=False)
```

time: 199 us -> 62.3 us (0.31)
  the two profiles are of different devices: /device:TPU:2 before, /device:TPU:1 now
where the time goes in v3:
time: 62.3 us; the launch traced here: 62.2 us
  Pallas kernels  61.4 us (99%)
  local copies, waits for them, and re-layouts  0.8 us (1%)
    pallas_call x1, Pallas kernels, on_device(): pl.pallas_call(kernel, out_shape=jax.ShapeDtypeStruct(values.shape, jnp.b...  61.4 us

profile of v3, /device:TPU:1, one launch (start us, length us, event | category | flops | bytes accessed | tf_op | source)
XLA Modules:
  0.0 62.2 jit_solution(11656722857042855162)
XLA Ops:
  0.0 61.4 %shard_map.46 = bf16[512,512]{1,0:T(8,128)(2,1)S(1)} custom-call(bf16[512,512]{1,0:T(8,128)(2,1)} %values_ref.1, s32[4,4]{1,0:T(4,128)} %tile_hbm.1, s32[4,4]{1,0:T(4,128)} %keep_hbm.1, s32[1,512]{1,0:T(1,128)} %bitcast.1), custom_call_target="tpu_custom_call" | custom-call | tf_op jit(solution)/shard_map/pallas_call | solution.py:430
  61.5 0.8 %copy.6 = bf16[512,512]{1,0:T(8,128)(2,1)} copy(bf16[512,512]{1,0:T(8,128)(2,1)S(1)} %shard_map.46) | data formatting | bytes 1048576

commit v4 on v3

--- a/solution.py
+++ b/solution.py
@@ -12,36 +12,36 @@
 NZ = 8
 MESH = pl.DeviceIdType.MESH
 
-OWN = [(0, 0, 0), (0, 0, 1), (0, 0, 2), (0, 0, 3)]
-XP = OWN + [(1, 0, 0), (1, 0, 2), (0, 1, 2), (0, 1, 3), (0, 3, 2), (0, 3, 3), (0, 2, 2), (0, 2, 3), (1, 1, 2), (1, 3, 2),
-            (1, 2, 2)]
-XM = OWN + [((-dx) % 4, dy, q ^ 1) for dx, dy, q in XP[4:]]
-YP = OWN + [(dy, dx, q ^ 2) for dx, dy, q in [XP[5], XP[4]] + XP[6:]]
-YM = OWN + [(dy, dx, q ^ 2) for dx, dy, q in [XM[5], XM[4]] + XM[6:]]
-ZP = [(d, q) for d in (0, 1, 2) for q in range(4)] + [(3, 0), (3, 1)]
-ZM = [(d, q) for d in (0, 7, 6) for q in range(4)] + [(5, 2), (5, 3)]
+OWN = [(0, 0, 0, 2), (0, 0, 2, 2)]
+XP = OWN + [(1, 0, 0, 1), (1, 0, 2, 1), (0, 1, 2, 2), (0, 3, 2, 2), (0, 2, 2, 2), (1, 1, 2, 1), (1, 3, 2, 1), (1, 2, 2, 1)]
+XM = OWN + [((-dx) % 4, dy, q ^ (n % 2), n) for dx, dy, q, n in XP[2:]]
+YP = OWN + [(dy, dx, q ^ 2, n) for dx, dy, q, n in [XP[3], XP[2]] + XP[4:]]
+YM = OWN + [(dy, dx, q ^ 2, n) for dx, dy, q, n in [XM[3], XM[2]] + XM[4:]]
+ZP = [(d, h) for d in (0, 1, 2) for h in (0, 1)] + [(3, 0)]
+ZM = [(d, h) for d in (0, 7, 6) for h in (0, 1)] + [(5, 1)]
 LINKS = {"xp": XP, "xm": XM, "yp": YP, "ym": YM, "zp": ZP, "zm": ZM}
-STEP = {"xp": (1, 0, 0), "xm": (3, 0, 0), "yp": (0, 1, 0), "ym": (0, 3, 0), "zp": (1, 0), "zm": (7, 0)}
-
-
-def land(link, chunk):
+BELOW = 176
+STEP = {"xp": (1, 0), "xm": (3, 0), "yp": (0, 1), "ym": (0, 3), "zp": (1,), "zm": (7,)}
+
+
+def land(link, piece):
     extent = 8 if link[0] == "z" else 4
-    moved = [(a + b) % extent for a, b in zip(chunk, STEP[link])]
-    return tuple(moved[:-1]) + (chunk[-1],)
-
-
-EVENT_OF_ROUND = [0, 0, 0, 0, 1, 1, 2, 2, 3, 3, 4, 4, 5, 6, 7]
+    step = STEP[link]
+    return tuple((a + b) % extent for a, b in zip(piece, step)) + piece[len(step) :]
+
+
+EVENT_OF_ROUND = [0, 0, 0, 0, 1, 2, 3, 4, 5, 6]
 EVENT_B = [0] * 16
 for _link in ("xp", "xm", "yp", "ym"):
     for _r, _c in enumerate(LINKS[_link]):
         _l = land(_link, _c)
         EVENT_B[_l[0] * 4 + _l[1]] = max(EVENT_B[_l[0] * 4 + _l[1]], EVENT_OF_ROUND[_r])
-EVENT_A = [0, 0, 1, 2, 3, 4, 6, 7, 8, 9, 5, 7, 3, 4, 1, 2]
+EVENT_A = [0, 0, 0, 1, 2, 3, 5, 6, 6, 7, 3, 4, 1, 2, 0, 0]
 
 
 def kernel(values_ref, tile_hbm, keep_hbm, thr_hbm, out_ref, raw, tile_ref, keep_ref, thr_ref, abuf, bbuf, acc, pbuf, sbuf,
-           vbuf, tbuf, raw_sem, send_xy, send_z, send_d, send_p, send_s, send_v, send_t, recv_b, recv_a, recv_d, recv_p,
-           recv_s, recv_v, recv_t, go, ready):
+           vbuf, tbuf, raw_sem, send_xy, send_z, send_d, send_p, send_s, send_v, send_t, recv_b, recv_a, recv_x, recv_d,
+           recv_p, recv_s, recv_v, recv_t, go, ready):
     row, col = lax.axis_index("row"), lax.axis_index("col")
     x, y, z, core = row // 4, row % 4, col // 2, col % 2
 
@@ -58,19 +58,15 @@
     partner = along(0, 1)
     plane = [peer[link] for link in ("xp", "xm", "yp", "ym")]
     line = [peer["zp"], peer["zm"]]
-    late_p = (z % 4) // 3
-    late_m = (3 - z % 4) // 3
-    late = late_p + late_m
+    late_p = z % 2
+    late_m = 1 - z % 2
 
     barrier = pltpu.get_barrier_semaphore()
     for to in plane:
         signal(barrier, (to[0], z * 2))
     signal(barrier, (row, ((z + 1) % 8) * 2 + late_p))
     signal(barrier, (row, ((z + 7) % 8) * 2 + late_m))
-
-    @pl.when(core == 1)
-    def _():
-        signal(barrier, partner)
+    signal(barrier, partner)
 
     tiles = pltpu.make_async_copy(tile_hbm, tile_ref, raw_sem.at[0])
     tiles.start()
@@ -105,8 +101,8 @@
     def arrived(ref, sem):
         remote(ref, ref, send_d.at[0], sem, partner).wait_recv()
 
-    def quarter(buf, slot, q):
-        return buf.at[slot, pl.ds(q * QR, QR), :]
+    def rows_of(slot, q, n):
+        return bbuf.at[slot, pl.ds(q * QR, n * QR), :]
 
     def half(slot, h):
         return abuf.at[slot, pl.ds(h * 256, 256), :]
@@ -120,13 +116,15 @@
         while more:
             more = False
             for link in nxt:
-                if nxt[link] == len(LINKS[link]) or LINKS[link][nxt[link]] not in have:
+                if nxt[link] == len(LINKS[link]):
                     continue
                 c = LINKS[link][nxt[link]]
+                if any((c[0], c[1], c[2] + k) not in have for k in range(c[3])):
+                    continue
                 to = land(link, c)
                 copy = remote(
-                    quarter(bbuf, c[0] * 4 + c[1], c[2]),
-                    quarter(bbuf, to[0] * 4 + to[1], to[2]),
+                    rows_of(c[0] * 4 + c[1], c[2], c[3]),
+                    rows_of(to[0] * 4 + to[1], to[2], to[3]),
                     send_xy.at[n_xy[0]],
                     recv_b.at[to[0] * 4 + to[1], to[2]],
                     peer[link],
@@ -140,48 +138,68 @@
     def along_xy(r):
         for link in nxt:
             to = land(link, LINKS[link][r])
-            arrived(quarter(bbuf, to[0] * 4 + to[1], to[2]), recv_b.at[to[0] * 4 + to[1], to[2]])
-            have.add(to)
+            arrived(rows_of(to[0] * 4 + to[1], to[2], to[3]), recv_b.at[to[0] * 4 + to[1], to[2]])
+            have.update((to[0], to[1], to[2] + k) for k in range(to[3]))
             advance()
 
-    def z_copy(link, c, slot):
+    def z_copy(link, r):
+        c = LINKS[link][r]
         to = land(link, c)
         return remote(
-            quarter(abuf, c[0] * 2, c[1]), quarter(abuf, to[0] * 2, to[1]), send_z.at[slot], recv_a.at[to[0], to[1]], peer[link]
+            half(c[0] * 2, c[1]),
+            half(to[0] * 2, to[1]),
+            send_z.at[r if link == "zp" else 7 + r],
+            recv_a.at[to[0], to[1]],
+            peer[link],
         )
 
+    def z_part(link, source, start, size, slot, sem):
+        rows = pl.ds(start, size)
+        return remote(abuf.at[source * 2, rows, :], abuf.at[8, rows, :], send_z.at[slot], sem, peer[link])
+
+    rest_rows = 256 - BELOW
+    parts_p = [z_part("zp", 3, 0, BELOW, 6, recv_a.at[4, 0]), z_part("zp", 3, BELOW, rest_rows, 14, recv_x)]
+    part_m = z_part("zm", 5, BELOW, rest_rows, 15, recv_x)
+
     def send_along_z(link, r):
-        z_copy(link, LINKS[link][r], r if link == "zp" else 14 + r).start()
+        z_copy(link, r).start()
+
+    def handed(dz, h):
+        return remote(half(dz * 2, h), half(dz * 2 + 1, h), send_d.at[dz * 2 + h], recv_d.at[dz, h], partner)
 
     def hand_over(dz, h):
-        copy = remote(half(dz * 2, h), half(dz * 2 + 1, h), send_d.at[dz * 2 + h], recv_d.at[dz, h], partner)
-        copy.start()
-        sent.append(copy)
+        handed(dz, h).start()
 
     def take_over(dz):
         for h in range(2):
             arrived(half(dz * 2 + 1, h), recv_d.at[dz, h])
 
-    def along_z(link, r):
+    def along_z(link, r, when=None):
+        if when is not None:
+            pl.when(when)(lambda: along_z(link, r))
+            return
         to = land(link, LINKS[link][r])
-        arrived(quarter(abuf, to[0] * 2, to[1]), recv_a.at[to[0], to[1]])
-        if to in LINKS[link]:
-            n = LINKS[link].index(to)
-            if link == "zp" and n == 13:
-                @pl.when(z != 7)
-                def _():
-                    send_along_z(link, n)
-
-            else:
-                send_along_z(link, n)
-        elif link == "zm" and to == (5, 1):
+        if to == (4, 0):
+            arrived(abuf.at[8, pl.ds(0, BELOW), :], recv_a.at[4, 0])
+            arrived(abuf.at[8, pl.ds(BELOW, rest_rows), :], recv_x)
+        else:
+            arrived(half(to[0] * 2, to[1]), recv_a.at[to[0], to[1]])
+        if (link, to) == ("zp", (3, 0)):
+            parts_p[0].start()
+
+            @pl.when(z != 7)
+            def _():
+                parts_p[1].start()
+
+        elif to in LINKS[link]:
+            send_along_z(link, LINKS[link].index(to))
+        elif (link, to) == ("zm", (5, 0)):
 
             @pl.when(z == 1)
             def _():
-                z_copy(link, to, 28).start()
-
-        if r % 2 == 1:
-            hand_over(to[0], to[1] // 2)
+                part_m.start()
+
+        hand_over(*to)
 
     def own_along_z(q):
         @pl.when(late_p == 0)
@@ -193,11 +211,11 @@
             send_along_z("zm", q)
 
     def across(when):
-        @pl.when(when & (late > 0))
+        @pl.when(when)
         def _():
             @pl.when(core == 1)
             def _():
-                pl.semaphore_wait(barrier, 2 * late)
+                pl.semaphore_wait(barrier, 3)
                 signal(go.at[1], partner)
 
             @pl.when(core == 0)
@@ -208,8 +226,8 @@
 
                 @pl.when(edge > 0)
                 def _():
-                    for r in range(4):
-                        send_along_z(link, r)
+                    for h in range(2):
+                        send_along_z(link, h)
 
     def greet(i, who):
         for to in who:
@@ -264,8 +282,8 @@
         lax.fori_loop(0, len(todo), step, 0)
 
     def to_plane(src, dst, send, recv):
-        for a in range(4):
-            for b in range(4):
+        for a in (2, 1, 3, 0):
+            for b in (2, 1, 3, 0):
                 if (a, b) != (0, 0):
                     copy = remote(src, dst.at[a * 4 + b], send.at[a * 4 + b], recv.at[a * 4 + b], at(a, b))
                     copy.start()
@@ -274,9 +292,16 @@
     tiles.wait()
     mask(0)
 
+    @pl.when(z == 7)
+    def _():
+        for i in range(1, 4):
+            mask(i)
+
+    across(z == 7)
+
     @pl.when(core == 0)
     def _():
-        pl.semaphore_wait(barrier, 13 - 2 * late)
+        pl.semaphore_wait(barrier, 11)
         signal(go.at[0], partner)
 
     @pl.when(core == 1)
@@ -285,13 +310,17 @@
 
     for i in range(4):
         if i:
-            mask(i)
+
+            @pl.when(z != 7)
+            def _():
+                mask(i)
+
         have.add((0, 0, i))
-        advance()
-        own_along_z(i)
         if i % 2:
+            advance()
+            own_along_z(i // 2)
             hand_over(0, i // 2)
-    across(z != 0)
+    across((z != 0) & (z != 7))
     greet(0, plane)
     acc[...] = jnp.zeros_like(acc)
     own_sum = jnp.zeros((1, BLK), jnp.float32)
@@ -314,18 +343,15 @@
     across(z == 0)
     greet(3, line)
     along_xy(0)
-    along_xy(1)
     along_z("zm", 0)
-    along_xy(2)
-    along_z("zm", 1)
-    along_z("zp", 0)
+    along_z("zp", 0, z != 0)
     met(3, line)
     greet(4, line)
-    along_xy(3)
-    along_z("zm", 2)
-    along_z("zp", 1)
-    take_over(0)
-    event(0)
+    along_xy(1)
+    along_z("zm", 1)
+    along_z("zp", 0, z == 0)
+    along_z("zp", 1, z != 0)
+    along_xy(2)
 
     @pl.when(is_root)
     def _():
@@ -335,15 +361,22 @@
             total = total + pbuf[k]
         sbuf[0] = total
 
-    for r in range(4, 15):
+    for r in range(3, 10):
+        if r == 9:
+            along_z("zm", 6)
+            along_z("zp", 6)
+            take_over(3)
         along_xy(r)
-        along_z("zm", r - 1)
-        if r < 14:
-            along_z("zp", r - 2)
-        if r == 5:
+        if r in (3, 4, 5, 6):
+            along_z("zm", r - 1)
+            along_z("zp", r - 2, z == 0)
+            along_z("zp", r - 1, z != 0)
+        if r == 8:
+            along_z("zp", 5, z == 0)
+        if r == 3:
             met(4, line)
             greet(5, line)
-        if r == 7:
+        if r == 4:
             met(5, line)
             for k in range(1, 16):
                 copy = remote(sbuf.at[0], sbuf.at[1], send_s.at[k], recv_s, along(k // 2, k % 2))
@@ -352,12 +385,10 @@
                 def _():
                     copy.start()
 
-        if r in (7, 11, 14):
-            for dz in {7: (1, 7), 11: (2, 6), 14: (3, 5)}[r]:
-                take_over(dz)
-        if r in (5, 7, 9, 11, 12, 13, 14):
-            event(EVENT_OF_ROUND[r])
-        if r == 11:
+        for dz in {3: (0, 7), 4: (1,), 5: (6,), 6: (2,), 7: (5,)}.get(r, ()):
+            take_over(dz)
+        event(EVENT_OF_ROUND[r])
+        if r == 6:
             @pl.when(slot != 0)
             def _():
                 arrived(sbuf.at[1], recv_s)
@@ -371,9 +402,6 @@
             own = jnp.dot(parts.astype(jnp.bfloat16), bbuf[0], preferred_element_type=jnp.float32)
             vbuf[0] = jnp.sum(own, axis=0, keepdims=True)
             to_plane(vbuf.at[0], vbuf, send_v, recv_v)
-    along_z("zp", 12)
-    along_z("zp", 13)
-    event(8)
     for fetch in rest:
         fetch.wait()
     col_means = vbuf[0]
@@ -382,7 +410,7 @@
         col_means = col_means + vbuf[k]
     cut = 0.125 * thr_ref[...].astype(jnp.float32) * (col_means / (BLK * 16))
     take_over(4)
-    event(9)
+    event(7)
 
     for j in range(4):
         total = jnp.zeros((1, TB), jnp.float32)
@@ -395,18 +423,22 @@
     to_plane(tbuf.at[0], tbuf, send_t, recv_t)
     for copy in sent:
         copy.wait_send()
+    for dz in range(8):
+        for h in range(2):
+            handed(dz, h).wait_send()
     for link in ("zp", "zm"):
-        for r in range(14):
-            if (link, r) != ("zp", 13):
-                z_copy(link, LINKS[link][r], r if link == "zp" else 14 + r).wait_send()
+        for r in range(7):
+            if (link, r) != ("zp", 6):
+                z_copy(link, r).wait_send()
+    parts_p[0].wait_send()
 
     @pl.when(z != 7)
     def _():
-        z_copy("zp", ZP[13], 13).wait_send()
+        parts_p[1].wait_send()
 
     @pl.when(z == 1)
     def _():
-        z_copy("zm", (5, 1), 28).wait_send()
+        part_m.wait_send()
 
     @pl.when(slot != 0)
     def _():
@@ -445,15 +477,16 @@
             pltpu.VMEM((16, 1, BLK), jnp.float32),
             pltpu.VMEM((16, 1, BLK), jnp.float32),
             dma((7,)),
-            dma((60,)),
-            dma((29,)),
+            dma((40,)),
+            dma((16,)),
             dma((16,)),
             dma,
             dma((16,)),
             dma((16,)),
             dma((16,)),
             dma((16, 4)),
-            dma((8, 4)),
+            dma((8, 2)),
+            dma,
             dma((8, 2)),
             dma((16,)),
             dma,

time: 62.3 us -> 60.7 us (0.974)
  Pallas kernels: 61.4 us -> 59.8 us
    pallas_call x1, Pallas kernels: 61.4 us -> 59.8 us  [on_device(): pl.pallas_call(kernel, out_shape=jax.ShapeDtypeStruct(values.shape, jnp.b...]
where the time goes in v4:
time: 60.7 us; the launch traced here: 60.6 us
  Pallas kernels  59.8 us (99%)
  local copies, waits for them, and re-layouts  0.8 us (1%)
    pallas_call x1, Pallas kernels, on_device(): pl.pallas_call(kernel, out_shape=jax.ShapeDtypeStruct(values.shape, jnp.b...  59.8 us

profile of v4, /device:TPU:1, one launch (start us, length us, event | category | flops | bytes accessed | tf_op | source)
XLA Modules:
  0.0 60.6 jit_solution(17093100974113991309)
XLA Ops:
  0.0 59.8 %shard_map.46 = bf16[512,512]{1,0:T(8,128)(2,1)S(1)} custom-call(bf16[512,512]{1,0:T(8,128)(2,1)} %values_ref.1, s32[4,4]{1,0:T(4,128)} %tile_hbm.1, s32[4,4]{1,0:T(4,128)} %keep_hbm.1, s32[1,512]{1,0:T(1,128)} %bitcast.1), custom_call_target="tpu_custom_call" | custom-call | tf_op jit(solution)/shard_map/pallas_call | solution.py:462
  59.8 0.8 %copy.6 = bf16[512,512]{1,0:T(8,128)(2,1)} copy(bf16[512,512]{1,0:T(8,128)(2,1)S(1)} %shard_map.46) | data formatting | bytes 1048576

commit v5 on v4

--- a/solution.py
+++ b/solution.py
@@ -12,15 +12,15 @@
 NZ = 8
 MESH = pl.DeviceIdType.MESH
 
-OWN = [(0, 0, 0, 2), (0, 0, 2, 2)]
-XP = OWN + [(1, 0, 0, 1), (1, 0, 2, 1), (0, 1, 2, 2), (0, 3, 2, 2), (0, 2, 2, 2), (1, 1, 2, 1), (1, 3, 2, 1), (1, 2, 2, 1)]
-XM = OWN + [((-dx) % 4, dy, q ^ (n % 2), n) for dx, dy, q, n in XP[2:]]
-YP = OWN + [(dy, dx, q ^ 2, n) for dx, dy, q, n in [XP[3], XP[2]] + XP[4:]]
-YM = OWN + [(dy, dx, q ^ 2, n) for dx, dy, q, n in [XM[3], XM[2]] + XM[4:]]
+UP, DOWN = [(0, 0, 0, 2), (0, 0, 2, 2)], [(0, 0, 2, 2), (0, 0, 0, 2)]
+XP = UP + [(1, 0, 0, 2), (0, 1, 2, 2), (0, 3, 2, 2), (0, 2, 2, 2), (1, 1, 2, 1), (1, 3, 2, 1), (1, 2, 2, 1)]
+XM = DOWN + [((-dx) % 4, dy, 2 if n == 2 else q ^ 1, n) for dx, dy, q, n in XP[2:]]
+YP = UP + [(0, 1, 0, 2)] + [(dy, dx, q ^ 2, n) for dx, dy, q, n in XP[3:]]
+YM = DOWN + [(0, 3, 2, 2)] + [(dy, dx, q ^ 2, n) for dx, dy, q, n in XM[3:]]
 ZP = [(d, h) for d in (0, 1, 2) for h in (0, 1)] + [(3, 0)]
 ZM = [(d, h) for d in (0, 7, 6) for h in (0, 1)] + [(5, 1)]
 LINKS = {"xp": XP, "xm": XM, "yp": YP, "ym": YM, "zp": ZP, "zm": ZM}
-BELOW = 176
+BELOW = 128
 STEP = {"xp": (1, 0), "xm": (3, 0), "yp": (0, 1), "ym": (0, 3), "zp": (1,), "zm": (7,)}
 
 
@@ -30,13 +30,13 @@
     return tuple((a + b) % extent for a, b in zip(piece, step)) + piece[len(step) :]
 
 
-EVENT_OF_ROUND = [0, 0, 0, 0, 1, 2, 3, 4, 5, 6]
+EVENT_OF_ROUND = [0, 0, 0, 1, 2, 3, 4, 5, 7]
 EVENT_B = [0] * 16
 for _link in ("xp", "xm", "yp", "ym"):
     for _r, _c in enumerate(LINKS[_link]):
         _l = land(_link, _c)
         EVENT_B[_l[0] * 4 + _l[1]] = max(EVENT_B[_l[0] * 4 + _l[1]], EVENT_OF_ROUND[_r])
-EVENT_A = [0, 0, 0, 1, 2, 3, 5, 6, 6, 7, 3, 4, 1, 2, 0, 0]
+EVENT_A = [0, 0, 0, 1, 2, 3, 5, 6, 6, 8, 3, 4, 1, 2, 0, 0]
 
 
 def kernel(values_ref, tile_hbm, keep_hbm, thr_hbm, out_ref, raw, tile_ref, keep_ref, thr_ref, abuf, bbuf, acc, pbuf, sbuf,
@@ -61,11 +61,13 @@
     late_p = z % 2
     late_m = 1 - z % 2
 
+    lead = 1 - z // 7
+    above, below = (z + 1) % 8, (z + 7) % 8
     barrier = pltpu.get_barrier_semaphore()
     for to in plane:
-        signal(barrier, (to[0], z * 2))
-    signal(barrier, (row, ((z + 1) % 8) * 2 + late_p))
-    signal(barrier, (row, ((z + 7) % 8) * 2 + late_m))
+        signal(barrier, (to[0], z * 2 + lead))
+    signal(barrier, (row, above * 2 + (late_p + 1 - above // 7) % 2))
+    signal(barrier, (row, below * 2 + (late_m + 1 - below // 7) % 2))
     signal(barrier, partner)
 
     tiles = pltpu.make_async_copy(tile_hbm, tile_ref, raw_sem.at[0])
@@ -210,15 +212,16 @@
         def _():
             send_along_z("zm", q)
 
+    def meet(when):
+        @pl.when(when & (core != lead))
+        def _():
+            pl.semaphore_wait(barrier, 3)
+            signal(go.at[1], partner)
+
     def across(when):
         @pl.when(when)
         def _():
-            @pl.when(core == 1)
-            def _():
-                pl.semaphore_wait(barrier, 3)
-                signal(go.at[1], partner)
-
-            @pl.when(core == 0)
+            @pl.when(core == lead)
             def _():
                 pl.semaphore_wait(go.at[1], 1)
 
@@ -297,14 +300,17 @@
         for i in range(1, 4):
             mask(i)
 
+    meet(z == 7)
     across(z == 7)
-
-    @pl.when(core == 0)
+    prompt = (z == 2) | ((z > 3) & (z < 7))
+    meet(prompt)
+
+    @pl.when(core == lead)
     def _():
         pl.semaphore_wait(barrier, 11)
         signal(go.at[0], partner)
 
-    @pl.when(core == 1)
+    @pl.when(core != lead)
     def _():
         pl.semaphore_wait(go.at[0], 1)
 
@@ -320,6 +326,7 @@
             advance()
             own_along_z(i // 2)
             hand_over(0, i // 2)
+    meet((z == 1) | (z == 3))
     across((z != 0) & (z != 7))
     greet(0, plane)
     acc[...] = jnp.zeros_like(acc)
@@ -340,6 +347,7 @@
     def _():
         to_root.start()
 
+    meet(z == 0)
     across(z == 0)
     greet(3, line)
     along_xy(0)
@@ -351,7 +359,6 @@
     along_z("zm", 1)
     along_z("zp", 0, z == 0)
     along_z("zp", 1, z != 0)
-    along_xy(2)
 
     @pl.when(is_root)
     def _():
@@ -361,22 +368,23 @@
             total = total + pbuf[k]
         sbuf[0] = total
 
-    for r in range(3, 10):
-        if r == 9:
+    for r in range(2, 9):
+        if r == 8:
             along_z("zm", 6)
             along_z("zp", 6)
             take_over(3)
+            event(6)
         along_xy(r)
-        if r in (3, 4, 5, 6):
-            along_z("zm", r - 1)
-            along_z("zp", r - 2, z == 0)
-            along_z("zp", r - 1, z != 0)
-        if r == 8:
+        if r in (2, 3, 4, 5):
+            along_z("zm", r)
+            along_z("zp", r - 1, z == 0)
+            along_z("zp", r, z != 0)
+        if r == 7:
             along_z("zp", 5, z == 0)
-        if r == 3:
+        if r == 2:
             met(4, line)
             greet(5, line)
-        if r == 4:
+        if r == 3:
             met(5, line)
             for k in range(1, 16):
                 copy = remote(sbuf.at[0], sbuf.at[1], send_s.at[k], recv_s, along(k // 2, k % 2))
@@ -385,10 +393,10 @@
                 def _():
                     copy.start()
 
-        for dz in {3: (0, 7), 4: (1,), 5: (6,), 6: (2,), 7: (5,)}.get(r, ()):
+        for dz in {2: (0, 7), 3: (1,), 4: (6,), 5: (2,), 6: (5,)}.get(r, ()):
             take_over(dz)
         event(EVENT_OF_ROUND[r])
-        if r == 6:
+        if r == 5:
             @pl.when(slot != 0)
             def _():
                 arrived(sbuf.at[1], recv_s)
@@ -410,7 +418,7 @@
         col_means = col_means + vbuf[k]
     cut = 0.125 * thr_ref[...].astype(jnp.float32) * (col_means / (BLK * 16))
     take_over(4)
-    event(7)
+    event(8)
 
     for j in range(4):
         total = jnp.zeros((1, TB), jnp.float32)

time: 60.7 us -> 60.4 us (level)
  no operation moved by 1% of the time
where the time goes in v5:
time: 60.4 us; the launch traced here: 60.3 us
  Pallas kernels  59.5 us (99%)
  local copies, waits for them, and re-layouts  0.8 us (1%)
    pallas_call x1, Pallas kernels, on_device(): pl.pallas_call(kernel, out_shape=jax.ShapeDtypeStruct(values.shape, jnp.b...  59.5 us

profile of v5, /device:TPU:1, one launch (start us, length us, event | category | flops | bytes accessed | tf_op | source)
XLA Modules:
  0.0 60.3 jit_solution(14899813116080923691)
XLA Ops:
  0.0 59.5 %shard_map.46 = bf16[512,512]{1,0:T(8,128)(2,1)S(1)} custom-call(bf16[512,512]{1,0:T(8,128)(2,1)} %values_ref.1, s32[4,4]{1,0:T(4,128)} %tile_hbm.1, s32[4,4]{1,0:T(4,128)} %keep_hbm.1, s32[1,512]{1,0:T(1,128)} %bitcast.1), custom_call_target="tpu_custom_call" | custom-call | tf_op jit(solution)/shard_map/pallas_call | solution.py:470
  59.5 0.8 %copy.6 = bf16[512,512]{1,0:T(8,128)(2,1)} copy(bf16[512,512]{1,0:T(8,128)(2,1)S(1)} %shard_map.46) | data formatting | bytes 1048576

commit v6 on v5

--- a/solution.py
+++ b/solution.py
@@ -396,7 +396,7 @@
         for dz in {2: (0, 7), 3: (1,), 4: (6,), 5: (2,), 6: (5,)}.get(r, ()):
             take_over(dz)
         event(EVENT_OF_ROUND[r])
-        if r == 5:
+        if r == 6:
             @pl.when(slot != 0)
             def _():
                 arrived(sbuf.at[1], recv_s)

time: 60.4 us -> 59.9 us (level)
  no operation moved by 1% of the time
where the time goes in v6:
time: 59.9 us; the launch traced here: 59.8 us
  Pallas kernels  59 us (98%)
  local copies, waits for them, and re-layouts  0.8 us (1%)
    pallas_call x1, Pallas kernels, on_device(): pl.pallas_call(kernel, out_shape=jax.ShapeDtypeStruct(values.shape, jnp.b...  59 us

profile of v6, /device:TPU:1, one launch (start us, length us, event | category | flops | bytes accessed | tf_op | source)
XLA Modules:
  0.0 59.8 jit_solution(5920404497574355448)
XLA Ops:
  0.0 59.0 %shard_map.46 = bf16[512,512]{1,0:T(8,128)(2,1)S(1)} custom-call(bf16[512,512]{1,0:T(8,128)(2,1)} %values_ref.1, s32[4,4]{1,0:T(4,128)} %tile_hbm.1, s32[4,4]{1,0:T(4,128)} %keep_hbm.1, s32[1,512]{1,0:T(1,128)} %bitcast.1), custom_call_target="tpu_custom_call" | custom-call | tf_op jit(solution)/shard_map/pallas_call | solution.py:470
  59.0 0.8 %copy.6 = bf16[512,512]{1,0:T(8,128)(2,1)} copy(bf16[512,512]{1,0:T(8,128)(2,1)S(1)} %shard_map.46) | data formatting | bytes 1048576

commit v7 on v6

--- a/solution.py
+++ b/solution.py
@@ -20,7 +20,7 @@
 ZP = [(d, h) for d in (0, 1, 2) for h in (0, 1)] + [(3, 0)]
 ZM = [(d, h) for d in (0, 7, 6) for h in (0, 1)] + [(5, 1)]
 LINKS = {"xp": XP, "xm": XM, "yp": YP, "ym": YM, "zp": ZP, "zm": ZM}
-BELOW = 128
+BELOW = 160
 STEP = {"xp": (1, 0), "xm": (3, 0), "yp": (0, 1), "ym": (0, 3), "zp": (1,), "zm": (7,)}
 
 
@@ -282,7 +282,10 @@
 
             return carry
 
-        lax.fori_loop(0, len(todo), step, 0)
+        if len(todo) == 1:
+            pl.when(todo[0][2])(lambda: multiply(*todo[0][:2]))
+        else:
+            lax.fori_loop(0, len(todo), step, 0)
 
     def to_plane(src, dst, send, recv):
         for a in (2, 1, 3, 0):

time: 59.9 us -> 59.9 us (level)
  no operation moved by 1% of the time
where the time goes in v7:
time: 59.9 us; the launch traced here: 59.8 us
  Pallas kernels  59 us (98%)
  local copies, waits for them, and re-layouts  0.8 us (1%)
    pallas_call x1, Pallas kernels, on_device(): pl.pallas_call(kernel, out_shape=jax.ShapeDtypeStruct(values.shape, jnp.b...  59 us

profile of v7, /device:TPU:1, one launch (start us, length us, event | category | flops | bytes accessed | tf_op | source)
XLA Modules:
  0.0 59.8 jit_solution(17621165240685024654)
XLA Ops:
  0.0 59.0 %shard_map.46 = bf16[512,512]{1,0:T(8,128)(2,1)S(1)} custom-call(bf16[512,512]{1,0:T(8,128)(2,1)} %values_ref.1, s32[4,4]{1,0:T(4,128)} %tile_hbm.1, s32[4,4]{1,0:T(4,128)} %keep_hbm.1, s32[1,512]{1,0:T(1,128)} %bitcast.1), custom_call_target="tpu_custom_call" | custom-call | tf_op jit(solution)/shard_map/pallas_call | solution.py:473
  59.0 0.8 %copy.6 = bf16[512,512]{1,0:T(8,128)(2,1)} copy(bf16[512,512]{1,0:T(8,128)(2,1)S(1)} %shard_map.46) | data formatting | bytes 1048576
